TPU v7x, 128 devices: a whole 4x4x4 slice. The times are simulated.
128 devices in a mesh: row: 2 (over core), col: 2 (over x_hi), depth: 32 (over z, y, x_lo).
Axes of the slice: x: 4 (x_hi: 2, x_lo: 2; x = x_hi * 2 + x_lo), y: 4, z: 4, core: 2. Of those that a mesh axis runs over, the one named last changes fastest.
Arguments:
- a_blocks: bfloat16 [64, 128, 4096], P('row', ('col', 'depth')), may hold values from -6 to 6
- a_mask: int32 [64, 128], P('row', ('col', 'depth')), may hold values 0 or 1
- a_row_ids: int32 [64], replicated, may hold values from 0 to 63, as said below
- a_col_ids: int32 [128], replicated, may hold values from 0 to 127, as said below
- b_matrix: bfloat16 [8192, 6144], P(('row', 'depth'), 'col'), may hold values from -0.0625 to 0.0625
- b_mask: int32 [128, 96], P(('row', 'depth'), 'col'), may hold values 0 or 1
Outputs:
- product: bfloat16 [4096, 6144], P(('row', 'depth'), 'col')
Inputs may be any that keep to these rules, and one draw needn't show every extreme that they name: `a_row_ids`: A permutation of the block rows; each aligned set of 32 entries holds at most 17 block rows r with the same r // 32, and every draw reaches 17. `a_col_ids`: A permutation of the block columns; entry v holds a block column k with (k // 2) % 32 == (v // 2) % 32.
All inputs are finite; a program needn't handle non-finite values. No bound on the sum of `a_mask` or of `b_mask` on one device may be relied on, other than what follows from the above.
Results may differ from a plain program's by a relative error of at most 0.001.
Values may be sent and summed in bfloat16 or wider, within the bound.
A program may use at most 64 MiB of HBM per device.

v0:
```python
import math

import jax
import jax.numpy as jnp
from jax import lax
from jax.sharding import PartitionSpec as P

LAYERS = 8


def partner(value, axis, stride):
    mask = 2**stride
    pairs = [(source, source ^ mask) for source in range(lax.axis_size(axis))]
    return lax.ppermute(value, axis, pairs)


def passed_along(block, axis, distance):
    devices = range(lax.axis_size(axis))
    route = [((i - distance) % len(devices), i) for i in devices]
    return lax.ppermute(block, axis, route)


def routes(row_ids, col_ids, grid_size, planes, plane_idx, rows_dev, cols_dev):
    owners = row_ids.reshape(grid_size, rows_dev)
    col_view = col_ids.reshape(grid_size, planes, cols_dev)
    columns = lax.dynamic_index_in_dim(col_view, plane_idx, 1, False)
    dest_row = owners // rows_dev
    sub_index = columns // cols_dev // planes
    dest_col = (sub_index[None, :, None, :] - dest_row[:, None, :, None]) % grid_size
    held_count = rows_dev * cols_dev
    destination = (dest_row[:, None, :, None] * grid_size + dest_col).reshape(
        grid_size, grid_size, held_count
    )
    target = (owners % rows_dev)[:, None, :, None] * cols_dev + (columns % cols_dev)[
        None, :, None, :
    ]
    target = target.reshape(grid_size, grid_size, held_count)
    matching = destination[..., :, None] == destination[..., None, :]
    earlier = jnp.tril(jnp.ones((held_count, held_count), jnp.bool_), -1)
    positions = jnp.sum(jnp.logical_and(matching, earlier), axis=-1)
    return (destination, target, positions)


def body(a_blocks, a_mask, a_row_ids, a_col_ids, b_matrix, b_mask):
    grid_size = lax.axis_size("row")
    planes = lax.axis_size("depth")
    my_row = lax.axis_index("row")
    my_col = lax.axis_index("col")
    my_depth = lax.axis_index("depth")
    layer_count = LAYERS
    group_count = planes // layer_count
    layer_bits = layer_count.bit_length() - 1
    group_bits = group_count.bit_length() - 1
    my_group = my_depth // layer_count
    my_layer = my_depth % layer_count
    rows_dev = a_blocks.shape[0]
    cols_dev = a_blocks.shape[1]
    block_side = math.isqrt(a_blocks.shape[2])
    held_count = rows_dev * cols_dev
    capacity = (rows_dev // grid_size + 1) * cols_dev
    slot_total = grid_size * grid_size * capacity
    destination, target, positions = routes(
        a_row_ids, a_col_ids, grid_size, planes, my_depth, rows_dev, cols_dev
    )
    own_dest = lax.dynamic_index_in_dim(
        lax.dynamic_index_in_dim(destination, my_row, 0, False), my_col, 0, False
    )
    own_pos = lax.dynamic_index_in_dim(
        lax.dynamic_index_in_dim(positions, my_row, 0, False), my_col, 0, False
    )
    slot_ids = own_dest * capacity + own_pos
    packing = (jnp.arange(slot_total, dtype=jnp.int32)[:, None] == slot_ids[None, :]).astype(
        jnp.bfloat16
    )
    payload = (a_blocks * a_mask[:, :, None].astype(jnp.bfloat16)).reshape(held_count, -1)
    outgoing = jnp.dot(packing, payload, preferred_element_type=jnp.float32).astype(jnp.bfloat16)
    incoming = lax.all_to_all(
        outgoing.reshape(grid_size * grid_size, capacity, -1),
        ("row", "col"),
        split_axis=0,
        concat_axis=0,
        tiled=True,
    )
    incoming = incoming.reshape(slot_total, -1)
    self_flat = my_row * grid_size + my_col
    for_here = destination == self_flat
    matched = jnp.logical_and(
        for_here[..., None, :],
        positions[..., None, :] == jnp.arange(capacity, dtype=jnp.int32)[:, None],
    )
    target_of = jnp.sum(jnp.where(matched, target[..., None, :], 0), axis=-1).reshape(-1)
    filled = jnp.any(matched, axis=-1).reshape(-1)
    placing = jnp.logical_and(
        target_of[None, :] == jnp.arange(held_count, dtype=jnp.int32)[:, None], filled[None, :]
    ).astype(jnp.bfloat16)
    placed = jnp.dot(placing, incoming, preferred_element_type=jnp.float32).astype(jnp.bfloat16)
    group_rows = rows_dev // group_count
    regroup = placed.reshape(group_count, group_rows, 1, cols_dev, block_side * block_side)
    for bit_pos in reversed(range(group_bits)):
        upper_bit = (my_group >> bit_pos) % 2 == 1
        half_size = regroup.shape[0] // 2
        lower_part = regroup[:half_size]
        upper_part = regroup[half_size:]
        kept_half = jnp.where(upper_bit, upper_part, lower_part)
        sent_half = jnp.where(upper_bit, lower_part, upper_part)
        received = partner(sent_half, "depth", bit_pos + layer_bits)
        first_piece = jnp.where(upper_bit, received, kept_half)
        second_piece = jnp.where(upper_bit, kept_half, received)
        regroup = jnp.stack([first_piece, second_piece], axis=3).reshape(
            half_size, group_rows, regroup.shape[2] * 2, cols_dev, -1
        )
    left_tile = regroup.reshape(
        group_rows, group_count * cols_dev, block_side, block_side
    ).transpose(0, 2, 1, 3)
    left_tile = left_tile.reshape(group_rows * block_side, group_count * cols_dev * block_side)
    col_width = b_matrix.shape[1]
    right_tile = b_matrix.reshape(
        cols_dev, block_side, col_width // block_side, block_side
    ) * b_mask[:, None, :, None].astype(jnp.bfloat16)
    right_tile = right_tile.reshape(cols_dev * block_side, col_width)
    for bit_pos in range(group_bits):
        upper_bit = (my_group >> bit_pos) % 2 == 1
        received = partner(right_tile, "depth", bit_pos + layer_bits)
        right_tile = jnp.where(
            upper_bit,
            jnp.concatenate([received, right_tile], axis=0),
            jnp.concatenate([right_tile, received], axis=0),
        )
    zeros_init = jnp.zeros((left_tile.shape[0], col_width), jnp.float32)
    bit_pos = 0
    shifted = passed_along(right_tile, "row", grid_size - (1 << bit_pos))
    right_tile = jnp.where((my_col >> bit_pos) % 2 == 1, shifted, right_tile)

    def advance(_, carried):
        running, left_now, right_now = carried
        running = running + jnp.dot(left_now, right_now, preferred_element_type=jnp.float32)
        left_now = passed_along(left_now, "col", grid_size - 1)
        right_now = passed_along(right_now, "row", grid_size - 1)
        return (running, left_now, right_now)

    partial_sum, left_tile, right_tile = lax.fori_loop(
        0, grid_size - 1, advance, (zeros_init, left_tile, right_tile)
    )
    partial_sum = partial_sum + jnp.dot(left_tile, right_tile, preferred_element_type=jnp.float32)
    running_sum = partial_sum
    for bit_pos in reversed(range(layer_bits)):
        upper_bit = (my_layer >> bit_pos) % 2 == 1
        half_size = running_sum.shape[0] // 2
        lower_part = running_sum[:half_size]
        upper_part = running_sum[half_size:]
        kept_half = jnp.where(upper_bit, upper_part, lower_part)
        sent_half = jnp.where(upper_bit, lower_part, upper_part)
        received = partner(sent_half, "depth", bit_pos)
        running_sum = kept_half + received
    return running_sum.astype(jnp.bfloat16)


def solution(mesh):
    return jax.shard_map(
        body,
        mesh=mesh,
        in_specs=(
            P("row", ("col", "depth"), None),
            P("row", ("col", "depth")),
            P(),
            P(),
            P(("row", "depth"), "col"),
            P(("row", "depth"), "col"),
        ),
        out_specs=P(("row", "depth"), "col"),
        check_vma=False,
    )
```

profile of v0, /device:TPU:0, one launch (start us, length us, event | category | flops | bytes accessed | tf_op | source)
XLA Modules:
  0.0 271.2 jit_solution(17860618003812462552)
XLA Ops:
  3.5 2.1 collective-permute-start.2
  5.6 17.5 %collective-permute-done.2 = bf16[128,3072]{1,0:T(8,128)(2,1)S(1)} collective-permute-done((bf16[128,3072]{1,0:T(8,128)(2,1)S(1)}, bf16[128,3072]{1,0:T(8,128)(2,1)S(1)}, u32[]{:S(2)}, u32[]{:S(2)}) %collective-permute-start.2) | collective-permute-done | bytes 786464 | tf_op jit(solution)/shard_map/ppermute | solution.py:14
  23.5 3.8 %collective-permute-start.3 = (bf16[256,3072]{1,0:T(8,128)(2,1)S(1)}, bf16[256,3072]{1,0:T(8,128)(2,1)}, u32[]{:S(2)}, u32[]{:S(2)}) collective-permute-start(bf16[256,3072]{1,0:T(8,128)(2,1)S(1)} %maximum_select_fusion.1), channel_id=1, source_target_pairs={{0,16},{1,17},{2,18},{3,19},{4,20},{5,21},{6,22},{7,23},{8,24},{9,... | collective-permute-start | bytes 4718600 | tf_op jit(solution)/shard_map/ppermute | solution.py:14
  27.7 2.4 broadcast_multiply_fusion
  30.0 30.9 %collective-permute-done.3 = bf16[256,3072]{1,0:T(8,128)(2,1)} collective-permute-done((bf16[256,3072]{1,0:T(8,128)(2,1)S(1)}, bf16[256,3072]{1,0:T(8,128)(2,1)}, u32[]{:S(2)}, u32[]{:S(2)}) %collective-permute-start.3) | collective-permute-done | bytes 1572896 | tf_op jit(solution)/shard_map/ppermute | solution.py:14
  60.9 3.3 %maximum_select_fusion = bf16[512,3072]{1,0:T(8,128)(2,1)S(1)} fusion(bf16[256,3072]{1,0:T(8,128)(2,1)} %copy-done.1, bf16[256,3072]{1,0:T(8,128)(2,1)} %collective-permute-done.3, pred[]{:T(512)S(6)} %eq.104), kind=kLoop, calls=%fused_computation.3 | loop fusion | flops 14155776 | bytes 6291457 | tf_op jit(solution)/shard_map/jit(_where)/select_n | solution.py:124
  64.8 2.0 reshape.320
  67.2 2.5 convolution_convert_fusion
  69.7 2.7 reshape.321
  72.4 4.4 %all-to-all-start = ((bf16[4,34,4096]{2,1,0:T(8,128)(2,1)}), bf16[4,34,4096]{2,1,0:T(8,128)(2,1)}, u32[]{:S(2)}, u32[]{:S(2)}) async-start(bf16[4,34,4096]{2,1,0:T(8,128)(2,1)} %reshape.321), calls=%async_computation | async-start | bytes 2621440 | tf_op jit(solution)/shard_map/all_to_all | solution.py:77
  77.6 18.1 %all-to-all-done = bf16[4,34,4096]{2,1,0:T(8,128)(2,1)} async-done(((bf16[4,34,4096]{2,1,0:T(8,128)(2,1)}), bf16[4,34,4096]{2,1,0:T(8,128)(2,1)}, u32[]{:S(2)}, u32[]{:S(2)}) %all-to-all-start) | async-done | bytes 1114144 | tf_op jit(solution)/shard_map/all_to_all | solution.py:77
  95.6 2.7 reshape.322
  98.3 1.6 convolution_convert_fusion.1
  102.8 3.2 %collective-permute-start = (bf16[2,8,1,2,4096]{4,1,3,0,2:T(8,128)(2,1)}, bf16[2,8,1,2,4096]{4,1,3,0,2:T(8,128)(2,1)}, u32[]{:S(2)}, u32[]{:S(2)}) collective-permute-start(bf16[2,8,1,2,4096]{4,1,3,0,2:T(8,128)(2,1)} %copy.30), channel_id=1, source_target_pairs={{0,16},{1,17},{2,18},{3,19},{4,20},{5,21},{6,22},{7,23},{8,24},{9,... | collective-permute-start | bytes 786440 | tf_op jit(solution)/shard_map/ppermute | solution.py:14
  107.1 2.0 broadcast_select_fusion
  109.1 3.2 %collective-permute-done = bf16[2,8,1,2,4096]{4,1,3,0,2:T(8,128)(2,1)} collective-permute-done((bf16[2,8,1,2,4096]{4,1,3,0,2:T(8,128)(2,1)}, bf16[2,8,1,2,4096]{4,1,3,0,2:T(8,128)(2,1)}, u32[]{:S(2)}, u32[]{:S(2)}) %collective-permute-start) | collective-permute-done | bytes 262176 | tf_op jit(solution)/shard_map/ppermute | solution.py:14
  113.6 1.4 collective-permute-start.1
  115.0 5.6 %collective-permute-done.1 = bf16[1,8,2,2,4096]{4,1,3,2,0:T(8,128)(2,1)S(1)} collective-permute-done((bf16[1,8,2,2,4096]{4,1,3,2,0:T(8,128)(2,1)S(1)}, bf16[1,8,2,2,4096]{4,1,3,2,0:T(8,128)(2,1)S(1)}, u32[]{:S(2)}, u32[]{:S(2)}) %collective-permute-start.1) | collective-permute-done | bytes 262176 | tf_op jit(solution)/shard_map/ppermute | solution.py:14
  123.2 1.6 collective-permute-start.5
  124.8 11.8 %collective-permute-done.5 = bf16[512,512]{1,0:T(8,128)(2,1)S(1)} collective-permute-done((bf16[512,512]{1,0:T(8,128)(2,1)S(1)}, bf16[512,512]{1,0:T(8,128)(2,1)S(1)}, u32[]{:S(2)}, u32[]{:S(2)}) %collective-permute-start.5) | collective-permute-done | bytes 524320 | tf_op jit(solution)/shard_map/while/body/eval_jaxpr/ppermute | solution.py:20
  136.6 3.7 %fusion.17 = f32[512,3072]{1,0:T(8,128)S(1)} fusion(bf16[512,512]{1,0:T(8,128)(2,1)S(1)} %collective-permute-done.5, bf16[512,3072]{1,0:T(8,128)(2,1)} %collective-permute-done.6), kind=kOutput, calls=%fused_computation.75 | convolution fusion | flops 1610612736 | bytes 9961472 | tf_op jit(solution)/shard_map/dot_general | solution.py:144
  140.3 3.7 %convolution_add_fusion = f32[512,3072]{1,0:T(8,128)S(1)} fusion(f32[512,3072]{1,0:T(8,128)S(1)} %fusion.17, bf16[512,512]{1,0:T(8,128)(2,1)S(1)} %reshape.323, bf16[512,3072]{1,0:T(8,128)(2,1)} %broadcast_select_fusion), kind=kOutput, calls=%fused_computation.1 | convolution fusion | flops 1612185600 | bytes 16252928 | tf_op jit(solution)/shard_map/while/body/eval_jaxpr/dot_general | solution.py:136
  144.4 2.2 copy-done
  146.6 3.2 %collective-permute-start.7 = (f32[256,3072]{1,0:T(8,128)S(1)}, f32[256,3072]{1,0:T(8,128)}, u32[]{:S(2)}, u32[]{:S(2)}) collective-permute-start(f32[256,3072]{1,0:T(8,128)S(1)} %slice_select_fusion), channel_id=1, source_target_pairs={{0,4},{1,5},{2,6},{3,7},{4,0},{5,1},{6,2},{7,3},{8,12},{9,13},{10,... | collective-permute-start | bytes 9437192 | tf_op jit(solution)/shard_map/ppermute | solution.py:14
  149.8 65.4 %collective-permute-done.7 = f32[256,3072]{1,0:T(8,128)} collective-permute-done((f32[256,3072]{1,0:T(8,128)S(1)}, f32[256,3072]{1,0:T(8,128)}, u32[]{:S(2)}, u32[]{:S(2)}) %collective-permute-start.7) | collective-permute-done | bytes 3145760 | tf_op jit(solution)/shard_map/ppermute | solution.py:14
  215.2 4.5 %select_add_fusion = f32[256,3072]{1,0:T(8,128)S(1)} fusion(f32[256,3072]{1,0:T(8,128)} %collective-permute-done.7, f32[512,3072]{1,0:T(8,128)} %copy-done, pred[]{:T(512)S(6)} %eq.102), kind=kLoop, calls=%fused_computation.4 | loop fusion | flops 1572864 | bytes 12582913 | tf_op jit(solution)/shard_map/add | solution.py:154
  219.7 1.3 slice_select_fusion.1
  221.1 1.6 collective-permute-start.8
  222.7 31.1 %collective-permute-done.8 = f32[128,3072]{1,0:T(8,128)} collective-permute-done((f32[128,3072]{1,0:T(8,128)}, f32[128,3072]{1,0:T(8,128)}, u32[]{:S(2)}, u32[]{:S(2)}) %collective-permute-start.8) | collective-permute-done | bytes 1572896 | tf_op jit(solution)/shard_map/ppermute | solution.py:14
  253.8 1.6 select_add_fusion.1
  255.5 1.5 collective-permute-start.9
  257.0 13.3 %collective-permute-done.9 = f32[64,3072]{1,0:T(8,128)S(1)} collective-permute-done((f32[64,3072]{1,0:T(8,128)S(1)}, f32[64,3072]{1,0:T(8,128)S(1)}, u32[]{:S(2)}, u32[]{:S(2)}) %collective-permute-start.9) | collective-permute-done | bytes 786464 | tf_op jit(solution)/shard_map/ppermute | solution.py:14
  (59 shorter events, 15.0 us)
Async XLA Ops:
  2.1 25.2 %copy-start.2 = (s32[128]{0:T(128)S(1)}, s32[128]{0:T(128)}, u32[]{:S(2)}) copy-start(s32[128]{0:T(128)} %param.9) | copy-start | bytes 1540
  2.1 25.3 %copy-start.4 = (s32[64]{0:T(128)S(1)}, s32[64]{0:T(128)}, u32[]{:S(2)}) copy-start(s32[64]{0:T(128)} %param.8) | copy-start | bytes 772
  2.1 25.4 %copy-start.3 = (s32[32,2]{0,1:T(2,128)S(1)}, s32[32,2]{0,1:T(2,128)}, u32[]{:S(2)}) copy-start(s32[32,2]{0,1:T(2,128)} %param.7) | copy-start | bytes 772
  3.5 19.6 %collective-permute-start.2 = (bf16[128,3072]{1,0:T(8,128)(2,1)S(1)}, bf16[128,3072]{1,0:T(8,128)(2,1)S(1)}, u32[]{:S(2)}, u32[]{:S(2)}) collective-permute-start(bf16[128,3072]{1,0:T(8,128)(2,1)S(1)} %mul.58), channel_id=1, source_target_pairs={{0,8},{1,9},{2,10},{3,11},{4,12},{5,13},{6,14},{7,15},{8,0},{9,1},... | collective-permute-start | bytes 2359304 | tf_op jit(solution)/shard_map/ppermute | solution.py:14
  23.5 6.5 %copy-start.1 = (bf16[256,3072]{1,0:T(8,128)(2,1)}, bf16[256,3072]{1,0:T(8,128)(2,1)S(1)}, u32[]{:S(2)}) copy-start(bf16[256,3072]{1,0:T(8,128)(2,1)S(1)} %maximum_select_fusion.1) | copy-start | bytes 4718596
  23.5 37.4 %collective-permute-start.3 = (bf16[256,3072]{1,0:T(8,128)(2,1)S(1)}, bf16[256,3072]{1,0:T(8,128)(2,1)}, u32[]{:S(2)}, u32[]{:S(2)}) collective-permute-start(bf16[256,3072]{1,0:T(8,128)(2,1)S(1)} %maximum_select_fusion.1), channel_id=1, source_target_pairs={{0,16},{1,17},{2,18},{3,19},{4,20},{5,21},{6,22},{7,23},{8,24},{9,... | collective-permute-start | bytes 4718600 | tf_op jit(solution)/shard_map/ppermute | solution.py:14
  64.2 42.9 %collective-permute-start.4 = (bf16[512,3072]{1,0:T(8,128)(2,1)S(1)}, bf16[512,3072]{1,0:T(8,128)(2,1)}, u32[]{:S(2)}, u32[]{:S(2)}) collective-permute-start(bf16[512,3072]{1,0:T(8,128)(2,1)S(1)} %maximum_select_fusion), channel_id=1, source_target_pairs={{64,0},{0,64},{65,1},{1,65},{66,2},{2,66},{67,3},{3,67},{68,4},{4,... | collective-permute-start | bytes 9437192 | tf_op jit(solution)/shard_map/ppermute | solution.py:20
  72.4 23.2 %all-to-all-start = ((bf16[4,34,4096]{2,1,0:T(8,128)(2,1)}), bf16[4,34,4096]{2,1,0:T(8,128)(2,1)}, u32[]{:S(2)}, u32[]{:S(2)}) async-start(bf16[4,34,4096]{2,1,0:T(8,128)(2,1)} %reshape.321), calls=%async_computation | async-start | bytes 2621440 | tf_op jit(solution)/shard_map/all_to_all | solution.py:77
  102.8 9.6 %collective-permute-start = (bf16[2,8,1,2,4096]{4,1,3,0,2:T(8,128)(2,1)}, bf16[2,8,1,2,4096]{4,1,3,0,2:T(8,128)(2,1)}, u32[]{:S(2)}, u32[]{:S(2)}) collective-permute-start(bf16[2,8,1,2,4096]{4,1,3,0,2:T(8,128)(2,1)} %copy.30), channel_id=1, source_target_pairs={{0,16},{1,17},{2,18},{3,19},{4,20},{5,21},{6,22},{7,23},{8,24},{9,... | collective-permute-start | bytes 786440 | tf_op jit(solution)/shard_map/ppermute | solution.py:14
  109.1 27.4 %collective-permute-start.6 = (bf16[512,3072]{1,0:T(8,128)(2,1)}, bf16[512,3072]{1,0:T(8,128)(2,1)}, u32[]{:S(2)}, u32[]{:S(2)}) collective-permute-start(bf16[512,3072]{1,0:T(8,128)(2,1)} %broadcast_select_fusion), channel_id=1, source_target_pairs={{64,0},{0,64},{65,1},{1,65},{66,2},{2,66},{67,3},{3,67},{68,4},{4,... | collective-permute-start | bytes 9437192 | tf_op jit(solution)/shard_map/while/body/eval_jaxpr/ppermute | solution.py:20
  113.6 7.0 %collective-permute-start.1 = (bf16[1,8,2,2,4096]{4,1,3,2,0:T(8,128)(2,1)S(1)}, bf16[1,8,2,2,4096]{4,1,3,2,0:T(8,128)(2,1)S(1)}, u32[]{:S(2)}, u32[]{:S(2)}) collective-permute-start(bf16[1,8,2,2,4096]{4,1,3,2,0:T(8,128)(2,1)S(1)} %select_bitcast_fusion), channel_id=1, source_target_pairs={{0,8},{1,9},{2,10},{3,11},{4,12},{5,13},{6,14},{7,15},{8,0},{9,1},... | collective-permute-start | bytes 786440 | tf_op jit(solution)/shard_map/ppermute | solution.py:14
  123.2 13.4 %collective-permute-start.5 = (bf16[512,512]{1,0:T(8,128)(2,1)S(1)}, bf16[512,512]{1,0:T(8,128)(2,1)S(1)}, u32[]{:S(2)}, u32[]{:S(2)}) collective-permute-start(bf16[512,512]{1,0:T(8,128)(2,1)S(1)} %reshape.323), channel_id=1, source_target_pairs={{32,0},{0,32},{33,1},{1,33},{34,2},{2,34},{35,3},{3,35},{36,4},{4,... | collective-permute-start | bytes 1572872 | tf_op jit(solution)/shard_map/while/body/eval_jaxpr/ppermute | solution.py:20
  144.0 2.6 copy-start
  146.6 68.6 %collective-permute-start.7 = (f32[256,3072]{1,0:T(8,128)S(1)}, f32[256,3072]{1,0:T(8,128)}, u32[]{:S(2)}, u32[]{:S(2)}) collective-permute-start(f32[256,3072]{1,0:T(8,128)S(1)} %slice_select_fusion), channel_id=1, source_target_pairs={{0,4},{1,5},{2,6},{3,7},{4,0},{5,1},{6,2},{7,3},{8,12},{9,13},{10,... | collective-permute-start | bytes 9437192 | tf_op jit(solution)/shard_map/ppermute | solution.py:14
  221.1 32.7 %collective-permute-start.8 = (f32[128,3072]{1,0:T(8,128)}, f32[128,3072]{1,0:T(8,128)}, u32[]{:S(2)}, u32[]{:S(2)}) collective-permute-start(f32[128,3072]{1,0:T(8,128)} %slice_select_fusion.1), channel_id=1, source_target_pairs={{0,2},{1,3},{2,0},{3,1},{4,6},{5,7},{6,4},{7,5},{8,10},{9,11},{10,... | collective-permute-start | bytes 4718600 | tf_op jit(solution)/shard_map/ppermute | solution.py:14
  255.5 14.8 %collective-permute-start.9 = (f32[64,3072]{1,0:T(8,128)S(1)}, f32[64,3072]{1,0:T(8,128)S(1)}, u32[]{:S(2)}, u32[]{:S(2)}) collective-permute-start(f32[64,3072]{1,0:T(8,128)S(1)} %slice_select_fusion.2), channel_id=1, source_target_pairs={{0,1},{1,0},{2,3},{3,2},{4,5},{5,4},{6,7},{7,6},{8,9},{9,8},{10,11... | collective-permute-start | bytes 2359304 | tf_op jit(solution)/shard_map/ppermute | solution.py:14
where the time goes:
time: 273 us; the launch traced here: 271 us
  waiting for transfers between devices  197 us (72%)
  starting transfers between devices  22.9 us (8%)
  other arithmetic  21.8 us (8%)
  local copies, waits for them, and re-layouts  17.9 us (7%)
  matrix products  11.5 us (4%)
    ppermute x7, waiting for transfers between devices, partner(): return lax.ppermute(value, axis, pairs)  167 us
    all_to_all x1, waiting for transfers between devices, body(): lax.all_to_all(outgoing.reshape(grid_size * grid_size, capacity, -1), ('r...  18.1 us
    ppermute x7, starting transfers between devices, partner(): return lax.ppermute(value, axis, pairs)  16.8 us
    ppermute x3, waiting for transfers between devices, passed_along(): return lax.ppermute(block, axis, route)  11.8 us
    add x2, other arithmetic, body(): running_sum = kept_half + received  6.15 us
  transfers between devices with their start and end apart: 11, of which 9 were waited for; matrix products, arithmetic and copies ran while one was open for 9% of the time, Pallas kernels for 0%

commit v1 on v0

v1 whole, which is shorter than its diff:
```python
import functools

import jax
import jax.numpy as jnp
from jax import lax
from jax.experimental import pallas as pl
from jax.experimental.pallas import tpu as pltpu
from jax.sharding import PartitionSpec as P

MESH = pl.DeviceIdType.MESH
CHUNKS = (384, 384, 384, 384)
GROUPS = ((2,), (1, 3), (0,))
HALF = 1536
F32 = jnp.float32
BF16 = jnp.bfloat16


def kernel(
    slot_ref, colid_ref, amask_ref, bmask_ref, a_ref, b_ref, out_ref,
    araw, tmp, bxs, pst, abuf, bbuf, rbuf, cp, rsin, rsout, rsfin, ilv, fin_s, fin_r,
    sx_s, sx_r, sa_s, sa_r, sb_s, sb_r, sc_s, sc_r,
):
    r = lax.axis_index("row")
    c = lax.axis_index("col")
    d = lax.axis_index("depth")
    z = lax.div(d, 8)
    y = lax.rem(lax.div(d, 2), 4)
    l = lax.rem(d, 2)
    x = c * 2 + l

    def depth_of(zz, yy, ll):
        return zz * 8 + yy * 2 + ll

    def dev_y(k):
        return (r, c, depth_of(z, lax.rem(y + k, 4), l))

    def dev_z(k):
        return (r, c, depth_of(lax.rem(z + k, 4), y, l))

    def dev_x(k):
        xx = lax.rem(x + k, 4)
        return (r, lax.div(xx, 2), depth_of(z, y, lax.rem(xx, 2)))

    sib = (1 - r, c, d)
    part = (r, c, depth_of(z, y, 1 - l))

    pending = []

    def rcopy(src, dst, ss, rs, dev):
        copy = pltpu.make_async_remote_copy(
            src_ref=src, dst_ref=dst, send_sem=ss, recv_sem=rs, device_id=dev, device_id_type=MESH
        )
        copy.start()
        pending.append(copy)
        return copy

    barrier = pltpu.get_barrier_semaphore()
    peers = [dev_y(1), dev_y(2), dev_y(3), dev_z(1), dev_z(3), dev_x(1), dev_x(3), sib]
    for peer in peers:
        pl.semaphore_signal(barrier, inc=1, device_id=peer, device_id_type=MESH)

    odd = lax.rem(lax.broadcasted_iota(jnp.int32, (64, 128), 0), 2) == 1

    def mask_a(u, _):
        factor = jnp.where(odd, amask_ref[1, u], amask_ref[0, u]).astype(F32)
        araw[r * 32 + u] = (a_ref[u].astype(F32) * factor).astype(BF16)
        return 0

    lax.fori_loop(0, 32, mask_a, 0, unroll=4)

    pl.semaphore_wait(barrier, len(peers))
    mine = pl.ds(r * 32, 32)
    ax = rcopy(araw.at[mine], araw.at[mine], sx_s, sx_r, sib)

    own_plane = y * 2 + l
    left_lane = lax.broadcasted_iota(jnp.int32, (64, 128), 1) < 64

    def mask_b(ch, half):
        start = sum(CHUNKS[:ch])
        for j in range(2):
            for t in range(CHUNKS[ch] // 128):
                col = half * HALF + (start + t * 128)
                block = half * (HALF // 64) + (start // 64 + t * 2)
                factor = jnp.where(left_lane, bmask_ref[j, block], bmask_ref[j, block + 1]).astype(F32)
                tile = b_ref[pl.ds(j * 64, 64), pl.ds(pl.multiple_of(col, 128), 128)].astype(F32)
                yield j, t, (tile * factor).astype(BF16)

    def prep_own(ch):
        for j, t, tile in mask_b(ch, l):
            bbuf[ch][own_plane, r * 2 + j, :, pl.ds(t * 128, 128)] = tile

    def prep_other(ch):
        for j, t, tile in mask_b(ch, 1 - l):
            bxs[ch][j, :, pl.ds(t * 128, 128)] = tile

    two = pl.ds(r * 2, 2)

    def piece(ch, k, lam):
        plane = lax.rem(y + k, 4) * 2 + (l if lam == 0 else 1 - l)
        return bbuf[ch].at[plane, two]

    B = {}

    def b_copy(ch, i, ref, dev):
        B[ch, i] = rcopy(ref, ref, sb_s.at[ch, i], sb_r.at[ch, i], dev)

    def b_pair(ch):
        B[ch, 0] = rcopy(bxs[ch], bbuf[ch].at[own_plane, two], sb_s.at[ch, 0], sb_r.at[ch, 0], part)

    def b_own(ch):
        b_copy(ch, 1, piece(ch, 0, 0), dev_y(1))
        b_copy(ch, 4, piece(ch, 0, 0), dev_y(3))

    def b_own_sib(ch):
        b_copy(ch, 7, piece(ch, 0, 0), sib)

    def b_other(ch):
        B[ch, 0].wait_recv()
        b_copy(ch, 2, piece(ch, 0, 1), dev_y(1))
        b_copy(ch, 5, piece(ch, 0, 1), dev_y(3))
        b_copy(ch, 8, piece(ch, 0, 1), sib)

    def b_mid(ch):
        B[ch, 1].wait_recv()
        b_copy(ch, 3, piece(ch, 3, 0), dev_y(1))
        b_copy(ch, 9, piece(ch, 3, 0), sib)
        B[ch, 4].wait_recv()
        b_copy(ch, 10, piece(ch, 1, 0), sib)
        B[ch, 5].wait_recv()
        b_copy(ch, 6, piece(ch, 1, 1), dev_y(3))
        b_copy(ch, 11, piece(ch, 1, 1), sib)
        B[ch, 2].wait_recv()
        b_copy(ch, 12, piece(ch, 3, 1), sib)

    def b_far(ch):
        B[ch, 3].wait_recv()
        b_copy(ch, 13, piece(ch, 2, 0), sib)
        B[ch, 6].wait_recv()
        b_copy(ch, 14, piece(ch, 2, 1), sib)

    def b_ready(ch):
        for i in range(7, 15):
            B[ch, i].wait_recv()
        for plane in range(8):
            for cc in range(2):
                for jj in range(2):
                    stored = (cc * 32 + z * 8 + plane) * 2 + jj
                    k = colid_ref[stored]
                    sel = lax.div(k, 64) * 2 + lax.rem(k, 2)
                    rbuf[ch][pl.ds((plane * 4 + cc * 2 + jj) * 64, 64), :] = bbuf[ch][plane, sel]

    def source(xx, yy):
        return (yy * 2 + lax.rem(xx, 2)) * 2 + lax.div(xx, 2)

    A = {}

    def a_copy(g, i, src, dst, dev):
        A[g, i] = rcopy(src, dst, sa_s.at[g, i], sa_r.at[g, i], dev)

    def a_prep(g):
        for k in (2, 1, 3, 0):
            yy = lax.rem(y + k, 4)
            n = 0
            for zr in GROUPS[g]:
                zz = lax.rem(z + zr, 4)
                for ll in range(2):
                    u = slot_ref[r * 32 + zz * 8 + yy * 2 + ll]
                    slot = (k * 8 + n) % 8
                    tmp[slot] = araw[u].astype(F32)
                    first = tmp[slot, pl.ds(0, 32, stride=2), :]
                    second = tmp[slot, pl.ds(1, 32, stride=2), :]
                    lane = left_lane[:32]
                    even = jnp.where(lane, first, pltpu.roll(second, 64, 1))
                    oddr = jnp.where(lane, pltpu.roll(first, 64, 1), second)
                    block = jnp.concatenate([even, oddr], axis=0).astype(BF16)
                    if k == 0:
                        abuf[g][source(x, y), pl.ds(n * 64, 64), :] = block
                    else:
                        pst[g][k - 1, pl.ds(n * 64, 64), :] = block
                    n += 1
            if k:
                a_copy(g, k - 1, pst[g].at[k - 1], abuf[g].at[source(x, y)], dev_y(k))
            else:
                a_ring(g, 0)

    def a_ring(g, k):
        if k:
            A[g, k - 1].wait_recv()
        ref = abuf[g].at[source(x, lax.rem(y + 4 - k, 4))]
        a_copy(g, 3 + k, ref, ref, dev_x(1))
        a_copy(g, 7 + k, ref, ref, dev_x(3))

    def a_rest(g):
        for k in (1, 3, 2):
            a_ring(g, k)

    def a_forward(g):
        for i, k in enumerate((0, 1)):
            A[g, 3 + k].wait_recv()
            ref = abuf[g].at[source(lax.rem(x + 3, 4), lax.rem(y + 4 - k, 4))]
            a_copy(g, 11 + i, ref, ref, dev_x(1))
        for i, k in enumerate((3, 2)):
            A[g, 7 + k].wait_recv()
            ref = abuf[g].at[source(lax.rem(x + 1, 4), lax.rem(y + 4 - k, 4))]
            a_copy(g, 13 + i, ref, ref, dev_x(3))

    def a_ready(g):
        for i in (5, 6, 7, 8, 11, 12, 13, 14):
            A[g, i].wait_recv()

    def multiply(ch, zr):
        g = [n for n, group in enumerate(GROUPS) if zr in group][0]
        rows = pl.ds(GROUPS[g].index(zr) * 128, 128)
        lhs = jnp.concatenate([abuf[g][i, rows, :] for i in range(16)], axis=1)
        total = jnp.dot(lhs, rbuf[ch][...], preferred_element_type=F32)
        cp[ch][zr, 0] = total[:64]
        cp[ch][zr, 1] = total[64:]

    C = {}

    def c_copy(ch, i, src, dst, dev):
        C[ch, i] = rcopy(src, dst, sc_s.at[ch, i], sc_r.at[ch, i], dev)

    def c_far(ch):
        multiply(ch, 2)
        c_copy(ch, 0, cp[ch].at[2, 0], rsin[ch].at[0], dev_z(1))
        c_copy(ch, 1, cp[ch].at[2, 1], rsin[ch].at[1], dev_z(3))

    def c_near(ch):
        multiply(ch, 1)
        c_copy(ch, 2, cp[ch].at[1, 1], rsin[ch].at[2], dev_z(1))
        multiply(ch, 3)
        c_copy(ch, 3, cp[ch].at[3, 0], rsin[ch].at[3], dev_z(3))

    def c_combine(ch):
        C[ch, 0].wait_recv()
        rsout[ch][0] = rsin[ch][0] + cp[ch][1, 0]
        c_copy(ch, 4, rsout[ch].at[0], rsfin[ch].at[0], dev_z(1))
        C[ch, 1].wait_recv()
        rsout[ch][1] = rsin[ch][1] + cp[ch][3, 1]
        c_copy(ch, 5, rsout[ch].at[1], rsfin[ch].at[1], dev_z(3))

    def c_own(ch):
        multiply(ch, 0)

    def columns(ch, half):
        return pl.ds(pl.multiple_of(half * HALF + sum(CHUNKS[:ch]), 128), CHUNKS[ch])

    def c_final(ch):
        C[ch, 3].wait_recv()
        C[ch, 4].wait_recv()
        value = cp[ch][0, 0] + rsin[ch][3] + rsfin[ch][0]
        for t in range(CHUNKS[ch] // 128):
            lanes = pl.ds(t * 128, 128)
            for p in range(2):
                ilv[ch][0, t, pl.ds(p, 32, stride=2), :] = value[p * 32 : p * 32 + 32, t * 128 : t * 128 + 128]
        C[ch, 2].wait_recv()
        C[ch, 5].wait_recv()
        value = cp[ch][0, 1] + rsin[ch][2] + rsfin[ch][1]
        for t in range(CHUNKS[ch] // 128):
            for p in range(2):
                ilv[ch][1, t, pl.ds(p, 32, stride=2), :] = value[p * 32 : p * 32 + 32, t * 128 : t * 128 + 128]
        for t in range(CHUNKS[ch] // 128):
            fin_s[ch][:, pl.ds(t * 128, 128)] = ilv[ch][1 - l, t].astype(BF16)
        c_copy(ch, 6, fin_s[ch], fin_r[ch], part)
        for t in range(CHUNKS[ch] // 128):
            col = l * HALF + (sum(CHUNKS[:ch]) + t * 128)
            out_ref[:, pl.ds(pl.multiple_of(col, 128), 128)] = ilv[ch][l, t].astype(BF16)

    def c_last(ch):
        C[ch, 6].wait_recv()
        out_ref[:, columns(ch, 1 - l)] = fin_r[ch][...]

    prep_own(0)
    b_own(0)
    prep_other(0)
    b_pair(0)
    ax.wait_recv()
    a_prep(0)
    b_own_sib(0)
    a_prep(1)
    prep_other(1)
    b_pair(1)
    a_rest(0)
    a_prep(2)
    prep_own(1)
    b_other(0)
    b_own(1)
    b_own_sib(1)
    a_rest(1)
    a_forward(0)
    prep_other(2)
    b_pair(2)
    b_mid(0)
    b_other(1)
    prep_own(2)
    b_own(2)
    b_own_sib(2)
    a_rest(2)
    prep_other(3)
    b_pair(3)
    prep_own(3)
    a_forward(1)
    b_far(0)
    b_mid(1)
    a_forward(2)
    b_other(2)
    b_own(3)
    b_own_sib(3)
    a_ready(0)
    b_ready(0)
    c_far(0)
    b_far(1)
    a_ready(1)
    c_near(0)
    b_mid(2)
    b_other(3)
    c_combine(0)
    b_ready(1)
    c_far(1)
    c_near(1)
    a_ready(2)
    c_own(0)
    c_final(0)
    b_far(2)
    b_mid(3)
    c_combine(1)
    b_ready(2)
    c_far(2)
    c_near(2)
    c_own(1)
    c_final(1)
    b_far(3)
    c_last(0)
    c_combine(2)
    b_ready(3)
    c_far(3)
    c_near(3)
    c_own(2)
    c_final(2)
    c_last(1)
    c_own(3)
    c_combine(3)
    c_last(2)
    c_final(3)
    c_last(3)
    for copy in pending:
        copy.wait_send()


def body(a_blocks, a_mask, a_row_ids, a_col_ids, b_matrix, b_mask):
    blocks = a_blocks.reshape(32, 2, 32, 128).transpose(0, 2, 1, 3).reshape(32, 64, 128)
    order = jnp.arange(64, dtype=jnp.int32)
    slots = jnp.sum(jnp.where(a_row_ids[None, :] == order[:, None], order[None, :], 0), axis=1)
    vmem = pl.BlockSpec(memory_space=pltpu.VMEM)
    smem = pl.BlockSpec(memory_space=pltpu.SMEM)
    n, groups = len(CHUNKS), len(GROUPS)
    rows = [128 * len(group) for group in GROUPS]
    dma = pltpu.SemaphoreType.DMA
    scratch = [
        pltpu.VMEM((64, 64, 128), BF16),
        pltpu.VMEM((8, 64, 128), F32),
        [pltpu.VMEM((2, 64, w), BF16) for w in CHUNKS],
        [pltpu.VMEM((3, m, 128), BF16) for m in rows],
        [pltpu.VMEM((16, m, 128), BF16) for m in rows],
        [pltpu.VMEM((8, 4, 64, w), BF16) for w in CHUNKS],
        [pltpu.VMEM((2048, w), BF16) for w in CHUNKS],
        [pltpu.VMEM((4, 2, 64, w), F32) for w in CHUNKS],
        [pltpu.VMEM((4, 64, w), F32) for w in CHUNKS],
        [pltpu.VMEM((2, 64, w), F32) for w in CHUNKS],
        [pltpu.VMEM((2, 64, w), F32) for w in CHUNKS],
        [pltpu.VMEM((2, w // 128, 64, 128), F32) for w in CHUNKS],
        [pltpu.VMEM((64, w), BF16) for w in CHUNKS],
        [pltpu.VMEM((64, w), BF16) for w in CHUNKS],
        dma, dma,
        dma((groups, 15)), dma((groups, 15)),
        dma((n, 15)), dma((n, 15)),
        dma((n, 7)), dma((n, 7)),
    ]
    return pl.pallas_call(
        kernel,
        out_shape=jax.ShapeDtypeStruct((64, 3072), BF16),
        in_specs=[smem, smem, smem, smem, vmem, vmem],
        out_specs=vmem,
        scratch_shapes=scratch,
        compiler_params=pltpu.CompilerParams(collective_id=0, has_side_effects=True),
        name="contract",
    )(slots, a_col_ids, a_mask.T, b_mask, blocks, b_matrix)


def solution(mesh):
    return jax.shard_map(
        body,
        mesh=mesh,
        in_specs=(
            P("row", ("col", "depth"), None),
            P("row", ("col", "depth")),
            P(),
            P(),
            P(("row", "depth"), "col"),
            P(("row", "depth"), "col"),
        ),
        out_specs=P(("row", "depth"), "col"),
        check_vma=False,
    )
```

time: 273 us -> 69.5 us (0.25)
  waiting for transfers between devices: 197 us -> 0 us
  Pallas kernels: 0 us -> 66.3 us
  starting transfers between devices: 22.9 us -> 0 us
  other arithmetic: 21.8 us -> 0.63 us
  local copies, waits for them, and re-layouts: 17.9 us -> 2.42 us
  matrix products: 11.5 us -> 0 us
    ppermute x10 -> x0, waiting for transfers between devices: 179 us -> none  [the longest x7 167 us: partner(): return lax.ppermute(value, axis, pairs)]
    pallas_call x0 -> x1, Pallas kernels: none -> 66.3 us  [body(): pl.pallas_call(kernel, out_shape=jax.ShapeDtypeStruct((64, 3072), BF16),...]
    ppermute x10 -> x0, starting transfers between devices: 18.5 us -> none  [the longest x7 16.8 us: partner(): return lax.ppermute(value, axis, pairs)]
    all_to_all x1 -> x0, waiting for transfers between devices: 18.1 us -> none  [body(): lax.all_to_all(outgoing.reshape(grid_size * grid_size, capacity, -1), ('r...]
    dot_general x4 -> x0, matrix products: 11.5 us -> none  [the longest x1 3.69 us: advance(): jnp.dot(left_now, right_now, preferred_element_type=jnp.float32)]
    select_n x9 -> x0, other arithmetic: 8.32 us -> none  [the longest x2 3.63 us: body(): jnp.where(upper_bit, jnp.concatenate([received, right_tile], axis=0), jnp...]
    reshape x6 -> x0, local copies, waits for them, and re-layouts: 8.23 us -> none  [the longest x1 2.7 us: body(): incoming = incoming.reshape(slot_total, -1)]
    add x5 -> x0, other arithmetic: 6.18 us -> none  [the longest x2 6.15 us: body(): running_sum = kept_half + received]
  transfers between devices with their start and end apart: 11 -> 0, of which waited for: 9 -> 0; matrix products, arithmetic and copies ran while one was open for 9% -> 0% of each run, Pallas kernels for 0% -> 0%
where the time goes in v1:
time: 69.5 us; the launch traced here: 69.4 us
  Pallas kernels  66.3 us (95%)
  local copies, waits for them, and re-layouts  2.42 us (3%)
    pallas_call x1, Pallas kernels, body(): pl.pallas_call(kernel, out_shape=jax.ShapeDtypeStruct((64, 3072), BF16),...  66.3 us
    unnamed x3, local copies, waits for them, and re-layouts  2.42 us

profile of v1, /device:TPU:0, one launch (start us, length us, event | category | flops | bytes accessed | tf_op | source)
XLA Modules:
  0.0 69.4 jit_solution(9469919797535638639)
XLA Ops:
  0.0 0.0 copy-start
  0.0 0.7 copy-done
  0.7 0.6 select_reduce_fusion.slot_ref
  1.3 66.3 %contract.1 = bf16[64,3072]{1,0:T(8,128)(2,1)} custom-call(s32[64]{0:T(128)} %select_reduce_fusion.slot_ref, s32[128]{0:T(128)} %colid_ref.1, s32[2,32]{1,0:T(2,128)} %bitcast.7, s32[2,48]{1,0:T(2,128)} %bmask_ref.1, bf16[32,64,128]{2,1,0:T(8,128)(2,1)} %bitcast.6, bf16[128,3072]{1,0:T(8,128)(2,1)} %b_ref.1), custom_call_target="tpu_custom_call" | custom-call | tf_op jit(solution)/shard_map/contract/pallas_call | solution.py:380
  67.6 1.8 %copy.10 = bf16[64,3072]{1,0:T(8,128)(2,1)} copy(bf16[64,3072]{1,0:T(8,128)(2,1)} %contract.1) | data formatting | bytes 786432
Async XLA Ops:
  0.0 0.7 copy-start

commit v2 on v0

v2 whole, which is shorter than its diff:
```python
import jax
import jax.numpy as jnp
from jax import lax
from jax.experimental import pallas as pl
from jax.experimental.pallas import tpu as pltpu
from jax.sharding import PartitionSpec as P

MESH = pl.DeviceIdType.MESH
CHUNKS = (256, 256, 256, 256, 256, 128, 128)
GROUPS = (((2, 0), (2, 1)), ((1, 1), (3, 0)), ((1, 0), (3, 1)), ((0, 0), (0, 1)))
BY_OTHER = (0, 1, 3)
A_DIRECT = ()
B_DIRECT = ()
LAST_DIRECT = (5, 6)
HALF = 1536
F32 = jnp.float32
BF16 = jnp.bfloat16

AX, B_PAIR, B_OWN, B_OTHER, B_MID, B_SIDE, B_FAR, B_READY, A_PREP, A_RING, A_FWD, A_READY = range(12)
C_FAR, C_NEAR, C_PRE, C_COMB, C_OWN, C_FINAL, C_LAST = range(12, 19)

ORDER = (
    (B_OWN, 3), (B_PAIR, 0), (AX,), (B_OWN, 0), (B_PAIR, 3), (A_PREP, 0, 2), (A_PREP, 0, 1), (A_PREP, 0, 3),
    (B_PAIR, 1), (A_PREP, 0, 0), (A_PREP, 1, 2), (A_PREP, 1, 1), (B_PAIR, 4), (A_PREP, 1, 3), (A_PREP, 2, 2),
    (B_MID, 3, 0), (A_PREP, 1, 0), (B_OTHER, 3), (A_RING, 0, 1), (B_OWN, 1), (A_RING, 0, 3), (A_RING, 0, 2),
    (B_OTHER, 1), (A_RING, 1, 2), (A_PREP, 2, 1), (A_RING, 1, 3), (A_RING, 1, 1), (B_MID, 3, 1), (A_FWD, 0, 1),
    (B_PAIR, 2), (A_FWD, 1, 0), (A_FWD, 0, 2), (A_PREP, 2, 3), (B_OTHER, 0), (A_FWD, 0, 0), (B_MID, 1, 1),
    (A_FWD, 0, 3), (B_MID, 1, 0), (A_FWD, 1, 3), (A_FWD, 1, 2), (A_PREP, 3, 2), (A_FWD, 1, 1), (A_PREP, 3, 1),
    (A_PREP, 2, 0), (A_PREP, 3, 3), (A_RING, 2, 2), (B_FAR, 3), (B_SIDE, 3), (A_RING, 2, 1), (B_SIDE, 1),
    (B_READY, 3), (A_RING, 2, 3), (B_PAIR, 5), (B_MID, 0, 0), (A_READY, 0), (B_MID, 0, 1), (B_OWN, 2), (C_FAR, 3),
    (A_FWD, 2, 0), (A_READY, 1), (B_FAR, 1), (B_PAIR, 6), (C_NEAR, 3), (A_FWD, 2, 1), (B_SIDE, 0), (A_FWD, 2, 2),
    (B_OTHER, 2), (B_READY, 1), (C_FAR, 1), (A_FWD, 2, 3), (C_NEAR, 1), (B_OWN, 4), (B_OTHER, 4), (A_RING, 3, 3),
    (A_PREP, 3, 0), (A_RING, 3, 2), (B_FAR, 0), (B_MID, 2, 0), (B_READY, 0), (C_FAR, 0), (C_NEAR, 0), (A_RING, 3, 1),
    (A_READY, 2), (C_PRE, 3), (C_PRE, 1), (B_MID, 2, 1), (C_COMB, 3, 0), (B_OTHER, 6), (C_COMB, 3, 1), (C_COMB, 1, 1),
    (B_OWN, 6), (A_FWD, 3, 3), (B_SIDE, 2), (A_FWD, 3, 0), (C_COMB, 1, 0), (C_PRE, 0), (A_FWD, 3, 1), (A_FWD, 3, 2),
    (B_MID, 4, 1), (B_MID, 4, 0), (C_COMB, 0, 1), (C_COMB, 0, 0), (B_FAR, 2), (B_OWN, 5), (B_OTHER, 5), (B_SIDE, 4),
    (B_READY, 2), (B_MID, 6, 0), (C_FAR, 2), (B_MID, 6, 1), (A_READY, 3), (C_OWN, 3), (B_SIDE, 6), (C_FINAL, 3),
    (C_OWN, 1), (B_FAR, 4), (C_OWN, 0), (C_NEAR, 2), (C_PRE, 2), (C_FINAL, 1), (B_MID, 5, 0), (B_MID, 5, 1),
    (B_READY, 4), (C_FAR, 4), (C_FINAL, 0), (B_FAR, 6), (C_COMB, 2, 1), (C_COMB, 2, 0), (B_SIDE, 5), (C_OWN, 2),
    (B_READY, 6), (C_OWN, 6), (C_PRE, 4), (C_FAR, 6), (C_PRE, 6), (B_FAR, 5), (C_NEAR, 4), (B_READY, 5), (C_FAR, 5),
    (C_COMB, 4, 0), (C_COMB, 4, 1), (C_OWN, 5), (C_OWN, 4), (C_FINAL, 2), (C_LAST, 1), (C_COMB, 6, 0), (C_COMB, 6, 1),
    (C_LAST, 3), (C_NEAR, 5), (C_PRE, 5), (C_COMB, 5, 1), (C_LAST, 0), (C_NEAR, 6), (C_COMB, 5, 0), (C_LAST, 2),
    (C_FINAL, 4), (C_FINAL, 5), (C_LAST, 4), (C_FINAL, 6),
)


def kernel(
    rowid_hbm, colid_hbm, amask_hbm, bmask_hbm, a_hbm, b_hbm, out_ref,
    rowid_ref, colid_ref, amask_ref, bmask_ref, a_ref, b_ref, in_sem, slotv, slot_ref, araw, tmp, bxs, pst, abuf, bbuf, rbuf, cp, rsin, rsout, rsfin, ilv, fin_s, fin_r, last,
    slot_sem, sx_s, sx_r, sa_s, sa_r, sb_s, sb_r, sc_s, sc_r, sf_s,
):
    r = lax.axis_index("row")
    c = lax.axis_index("col")
    d = lax.axis_index("depth")
    z = lax.div(d, 8)
    y = lax.rem(lax.div(d, 2), 4)
    l = lax.rem(d, 2)
    x = c * 2 + l
    x_part = c * 2 + (1 - l)
    x_other = lax.rem(x + 3 + 2 * l, 4)
    x_far = lax.rem(x + 2, 4)

    def dev(xx, yy, zz):
        return (r, lax.div(xx, 2), zz * 8 + yy * 2 + lax.rem(xx, 2))

    def dev_y(k):
        return dev(x, lax.rem(y + k, 4), z)

    def dev_z(k):
        return dev(x, y, lax.rem(z + k, 4))

    part, other, far = dev(x_part, y, z), dev(x_other, y, z), dev(x_far, y, z)
    sib = (1 - r, c, d)
    def rcopy(src, dst, ss, rs, target):
        copy = pltpu.make_async_remote_copy(
            src_ref=src, dst_ref=dst, send_sem=ss, recv_sem=rs, device_id=target, device_id_type=MESH
        )
        copy.start()
        return copy

    def bytes_of(ref, ss, rs):
        return pltpu.make_async_remote_copy(
            src_ref=ref, dst_ref=ref, send_sem=ss, recv_sem=rs, device_id=sib, device_id_type=MESH
        )

    barrier = pltpu.get_barrier_semaphore()
    peers = [dev_y(1), dev_y(2), dev_y(3), dev_z(1), dev_z(3), part, other, sib] + ([far] if A_DIRECT else [])
    if LAST_DIRECT:
        peers += [dev(x_part, y, lax.rem(z + 1, 4)), dev(x_part, y, lax.rem(z + 3, 4))]
    for peer in peers:
        pl.semaphore_signal(barrier, inc=1, device_id=peer, device_id_type=MESH)

    inputs = ((rowid_hbm, rowid_ref), (amask_hbm, amask_ref), (a_hbm, a_ref), (bmask_hbm, bmask_ref), (b_hbm, b_ref), (colid_hbm, colid_ref))
    loads = [pltpu.make_async_copy(src, dst, in_sem.at[i]) for i, (src, dst) in enumerate(inputs)]
    for load in loads:
        load.start()

    loads[0].wait()
    place = lax.broadcasted_iota(jnp.int32, (8, 128), 1)
    slots = jnp.zeros((8, 128), jnp.int32)
    for u in range(64):
        slots = jnp.where(place == rowid_ref[u], u, slots)
    slotv[...] = slots

    odd = lax.rem(lax.broadcasted_iota(jnp.int32, (64, 128), 0), 2) == 1

    def mask_a(u, _):
        factor = jnp.where(odd, amask_ref[1, u], amask_ref[0, u]).astype(F32)
        araw[r * 32 + u] = (a_ref[u].astype(F32) * factor).astype(BF16)
        return 0

    loads[1].wait()
    loads[2].wait()
    lax.fori_loop(0, 32, mask_a, 0, unroll=4)
    to_smem = pltpu.make_async_copy(slotv, slot_ref, slot_sem)
    to_smem.start()

    for load in loads[3:]:
        load.wait()
    pl.semaphore_wait(barrier, len(peers))
    left_lane = lax.broadcasted_iota(jnp.int32, (64, 128), 1) < 64
    own_plane = y * 2 + l
    two = pl.ds(r * 2, 2)
    exchange = []

    def ax():
        mine = pl.ds(r * 32, 32)
        exchange.append(rcopy(araw.at[mine], araw.at[mine], sx_s, sx_r, sib))
        to_smem.wait()

    def mask_b(ch, half):
        start = sum(CHUNKS[:ch])
        for j in range(2):
            for t in range(CHUNKS[ch] // 128):
                col = half * HALF + (start + t * 128)
                block = half * (HALF // 64) + (start // 64 + t * 2)
                factor = jnp.where(left_lane, bmask_ref[j, block], bmask_ref[j, block + 1]).astype(F32)
                tile = b_ref[pl.ds(j * 64, 64), pl.ds(pl.multiple_of(col, 128), 128)].astype(F32)
                yield j, t, (tile * factor).astype(BF16)

    def piece(ch, k, lam):
        plane = lax.rem(y + k, 4) * 2 + (l if lam == 0 else 1 - l)
        return bbuf[ch].at[plane, two]

    def b_copy(ch, i, ref, target):
        rcopy(ref, ref, sb_s.at[ch], sb_r.at[ch, i], target)

    def b_wait(ch, i, pieces):
        bytes_of(rbuf[ch].at[pl.ds(0, 128 * pieces)], sb_s.at[ch], sb_r.at[ch, i]).wait_recv()

    def b_pair(ch):
        for j, t, tile in mask_b(ch, 1 - l):
            bxs[ch][j, :, pl.ds(t * 128, 128)] = tile
        rcopy(bxs[ch], bbuf[ch].at[own_plane, two], sb_s.at[ch], sb_r.at[ch, 0], part)

    def b_own(ch):
        for j, t, tile in mask_b(ch, l):
            bbuf[ch][own_plane, r * 2 + j, :, pl.ds(t * 128, 128)] = tile
        b_copy(ch, 1, piece(ch, 0, 0), dev_y(1))
        b_copy(ch, 3, piece(ch, 0, 0), dev_y(3))
        if ch in B_DIRECT:
            b_copy(ch, 4, piece(ch, 0, 0), dev_y(2))
        b_copy(ch, 5, piece(ch, 0, 0), sib)

    def b_other(ch):
        b_wait(ch, 0, 1)
        b_copy(ch, 3, piece(ch, 0, 1), dev_y(1))
        b_copy(ch, 2, piece(ch, 0, 1), dev_y(3))
        if ch in B_DIRECT:
            b_copy(ch, 4, piece(ch, 0, 1), dev_y(2))
        b_copy(ch, 5, piece(ch, 0, 1), sib)

    def b_mid(ch, lam):
        b_wait(ch, 1 + lam, 1)
        ref = piece(ch, 3 - 2 * lam, lam)
        if ch not in B_DIRECT:
            b_copy(ch, 4, ref, dev_y(1 + 2 * lam))
        b_copy(ch, 5, ref, sib)

    def b_side(ch):
        b_wait(ch, 3, 2)
        b_copy(ch, 5, piece(ch, 1, 0), sib)
        b_copy(ch, 5, piece(ch, 3, 1), sib)

    def b_far(ch):
        b_wait(ch, 4, 2)
        b_copy(ch, 5, piece(ch, 2, 0), sib)
        b_copy(ch, 5, piece(ch, 2, 1), sib)

    def b_ready(ch):
        b_wait(ch, 5, 8)
        for plane in range(8):
            for cc in range(2):
                for jj in range(2):
                    k = colid_ref[(cc * 32 + z * 8 + plane) * 2 + jj]
                    sel = lax.div(k, 64) * 2 + lax.rem(k, 2)
                    rbuf[ch][pl.ds((plane * 4 + cc * 2 + jj) * 64, 64), :] = bbuf[ch][plane, sel]

    def source(xx, yy):
        return (yy * 2 + lax.rem(xx, 2)) * 2 + lax.div(xx, 2)

    def held(g, xx, k):
        return abuf[g].at[source(xx, lax.rem(y + 4 - k, 4))]

    def a_copy(g, i, src, dst, target):
        rcopy(src, dst, sa_s.at[g], sa_r.at[g, i], target)

    def a_wait(g, i, pieces):
        bytes_of(abuf[g].at[pl.ds(0, pieces)], sa_s.at[g], sa_r.at[g, i]).wait_recv()

    def a_prep(g, k):
        if (g, k) == (0, 2):
            exchange[0].wait_recv()
        yy = lax.rem(y + k, 4)
        for n, (zr, ll) in enumerate(GROUPS[g]):
            zz = lax.rem(z + zr, 4)
            u = slot_ref[0, r * 32 + zz * 8 + yy * 2 + ll]
            slot = (k * 2 + n) % 8
            tmp[slot] = araw[u].astype(F32)
            first = tmp[slot, pl.ds(0, 32, stride=2), :]
            second = tmp[slot, pl.ds(1, 32, stride=2), :]
            lane = left_lane[:32]
            even = jnp.where(lane, first, pltpu.roll(second, 64, 1))
            oddr = jnp.where(lane, pltpu.roll(first, 64, 1), second)
            block = jnp.concatenate([even, oddr], axis=0).astype(BF16)
            if k == 0:
                abuf[g][source(x, y), pl.ds(n * 64, 64), :] = block
            else:
                pst[g][k - 1, pl.ds(n * 64, 64), :] = block
        if k:
            a_copy(g, k - 1, pst[g].at[k - 1], abuf[g].at[source(x, y)], dev_y(k))
        else:
            a_send(g, 0)

    def a_send(g, k):
        ref = held(g, x, k)
        onward = g not in A_DIRECT
        a_copy(g, 3 + k if onward and k in BY_OTHER else 7, ref, ref, part)
        a_copy(g, 3 + k if onward and k not in BY_OTHER else 7, ref, ref, other)
        if not onward:
            a_copy(g, 7, ref, ref, far)

    def a_ring(g, k):
        a_wait(g, k - 1, 1)
        a_send(g, k)

    def a_fwd(g, k):
        a_wait(g, 3 + k, 1)
        via, target = (x_part, other) if k in BY_OTHER else (x_other, part)
        ref = held(g, via, k)
        a_copy(g, 7, ref, ref, target)

    def a_ready(g):
        a_wait(g, 7, 12 if g in A_DIRECT else 8)

    def multiply(ch, g):
        lhs = jnp.concatenate([abuf[g][i] for i in range(16)], axis=1)
        total = jnp.dot(lhs, rbuf[ch][...], preferred_element_type=F32)
        for n, unit in enumerate(GROUPS[g]):
            cp[ch][unit] = total[n * 64 : n * 64 + 64]

    def c_copy(ch, i, src, dst, target):
        rcopy(src, dst, sc_s.at[ch], sc_r.at[ch, i], target)

    def c_wait(ch, i, ref):
        bytes_of(ref, sc_s.at[ch], sc_r.at[ch, i]).wait_recv()

    def last_copy(ch, src, kind, target):
        rcopy(src, last[LAST_DIRECT.index(ch)].at[kind, l], sc_s.at[ch], sc_r.at[ch, 2], target)

    def c_far(ch):
        multiply(ch, 0)
        c_copy(ch, 0, cp[ch].at[2, 0], rsin[ch].at[0], dev_z(1))
        c_copy(ch, 1, cp[ch].at[2, 1], rsin[ch].at[1], dev_z(3))

    def c_near(ch):
        multiply(ch, 1)
        if ch in LAST_DIRECT:
            last_copy(ch, cp[ch].at[1, 1], 0, dev(c * 2 + 1, y, lax.rem(z + 1, 4)))
            last_copy(ch, cp[ch].at[3, 0], 0, dev(c * 2, y, lax.rem(z + 3, 4)))
        else:
            c_copy(ch, 2, cp[ch].at[1, 1], rsin[ch].at[2], dev_z(1))
            c_copy(ch, 2, cp[ch].at[3, 0], rsin[ch].at[3], dev_z(3))

    def c_pre(ch):
        multiply(ch, 2)

    def c_comb(ch, n):
        c_wait(ch, n, cp[ch].at[0, 0])
        rsout[ch][n] = rsin[ch][n] + cp[ch][1 + 2 * n, n]
        if ch in LAST_DIRECT:
            last_copy(ch, rsout[ch].at[n], 1, dev(c * 2 + n, y, lax.rem(z + 1 + 2 * n, 4)))
            return
        c_copy(ch, 2, rsout[ch].at[n], rsfin[ch].at[n], dev_z(1 + 2 * n))

    def c_own(ch):
        multiply(ch, 3)
        if ch in LAST_DIRECT:
            rcopy(cp[ch].at[0, 1 - l], last[LAST_DIRECT.index(ch)].at[2, l], sf_s.at[1 + LAST_DIRECT.index(ch)], sc_r.at[ch, 3], part)

    def out_half(ch, s, h):
        for t in range(CHUNKS[ch] // 128):
            col = s * HALF + (sum(CHUNKS[:ch]) + t * 128)
            out_ref[:, pl.ds(pl.multiple_of(col, 128), 128)] = ilv[ch][h, t].astype(BF16)

    def interleave(ch, h, value):
        for t in range(CHUNKS[ch] // 128):
            for p in range(2):
                half = value[p * 32 : p * 32 + 32, t * 128 : t * 128 + 128]
                ilv[ch][h, t, pl.ds(p, 32, stride=2), :] = half

    def c_final_direct(ch):
        at = LAST_DIRECT.index(ch)
        c_wait(ch, 2, cp[ch].at[pl.ds(0, 2)])
        c_wait(ch, 3, cp[ch].at[0, 0])
        for n, s in enumerate((l, 1 - l)):
            own = last[at][2, s] if n else cp[ch][0, l]
            interleave(ch, n, own + last[at][0, s] + last[at][1, s])
            out_half(ch, s, n)

    def c_final(ch):
        if ch in LAST_DIRECT:
            return c_final_direct(ch)
        c_wait(ch, 2, cp[ch].at[pl.ds(0, 2)])
        for h in range(2):
            value = cp[ch][0, h] + rsin[ch][3 - h] + rsfin[ch][h]
            interleave(ch, h, value)
        for t in range(CHUNKS[ch] // 128):
            fin_s[ch][:, pl.ds(t * 128, 128)] = ilv[ch][1 - l, t].astype(BF16)
        rcopy(fin_s[ch], fin_r[ch], sf_s.at[0], sc_r.at[ch, 3], part)
        out_half(ch, l, l)

    def c_last(ch):
        c_wait(ch, 3, fin_r[ch])
        col = (1 - l) * HALF + sum(CHUNKS[:ch])
        out_ref[:, pl.ds(pl.multiple_of(col, 128), CHUNKS[ch])] = fin_r[ch][...]

    steps = (
        ax, b_pair, b_own, b_other, b_mid, b_side, b_far, b_ready, a_prep, a_ring, a_fwd, a_ready,
        c_far, c_near, c_pre, c_comb, c_own, c_final, c_last,
    )
    for step, *where in ORDER:
        steps[step](*where)

    exchange[0].wait_send()
    for g in range(len(GROUPS)):
        bytes_of(abuf[g].at[pl.ds(0, 15)], sa_s.at[g], sa_r.at[g, 0]).wait_send()
    for ch in range(len(CHUNKS)):
        bytes_of(rbuf[ch].at[pl.ds(0, 1920)], sb_s.at[ch], sb_r.at[ch, 0]).wait_send()
        bytes_of(cp[ch].at[pl.ds(0, 3)], sc_s.at[ch], sc_r.at[ch, 0]).wait_send()
    for at, ch in enumerate(LAST_DIRECT):
        bytes_of(cp[ch].at[0, 0], sf_s.at[1 + at], sc_r.at[ch, 3]).wait_send()
    width = sum(CHUNKS[ch] for ch in range(len(CHUNKS)) if ch not in LAST_DIRECT)
    bytes_of(b_ref.at[pl.ds(0, 64), pl.ds(0, width)], sf_s.at[0], sc_r.at[0, 3]).wait_send()


def body(a_blocks, a_mask, a_row_ids, a_col_ids, b_matrix, b_mask):
    blocks = a_blocks.reshape(32, 2, 32, 128).transpose(0, 2, 1, 3).reshape(32, 64, 128)
    vmem = pl.BlockSpec(memory_space=pltpu.VMEM)
    hbm = pl.BlockSpec(memory_space=pltpu.HBM)
    n, groups = len(CHUNKS), len(GROUPS)
    rows = [128] * groups
    dma = pltpu.SemaphoreType.DMA
    scratch = [
        pltpu.SMEM((64,), jnp.int32),
        pltpu.SMEM((128,), jnp.int32),
        pltpu.SMEM((2, 32), jnp.int32),
        pltpu.SMEM((2, 48), jnp.int32),
        pltpu.VMEM((32, 64, 128), BF16),
        pltpu.VMEM((128, 3072), BF16),
        dma((6,)),
        pltpu.VMEM((8, 128), jnp.int32),
        pltpu.SMEM((8, 128), jnp.int32),
        pltpu.VMEM((64, 64, 128), BF16),
        pltpu.VMEM((8, 64, 128), F32),
        [pltpu.VMEM((2, 64, w), BF16) for w in CHUNKS],
        [pltpu.VMEM((3, m, 128), BF16) for m in rows],
        [pltpu.VMEM((16, m, 128), BF16) for m in rows],
        [pltpu.VMEM((8, 4, 64, w), BF16) for w in CHUNKS],
        [pltpu.VMEM((2048, w), BF16) for w in CHUNKS],
        [pltpu.VMEM((4, 2, 64, w), F32) for w in CHUNKS],
        [pltpu.VMEM((4, 64, w), F32) for w in CHUNKS],
        [pltpu.VMEM((2, 64, w), F32) for w in CHUNKS],
        [pltpu.VMEM((2, 64, w), F32) for w in CHUNKS],
        [pltpu.VMEM((2, w // 128, 64, 128), F32) for w in CHUNKS],
        [pltpu.VMEM((64, w), BF16) for w in CHUNKS],
        [pltpu.VMEM((64, w), BF16) for w in CHUNKS],
        [pltpu.VMEM((3, 2, 64, CHUNKS[ch]), F32) for ch in LAST_DIRECT],
        dma, dma, dma,
        dma((groups,)), dma((groups, 8)),
        dma((n,)), dma((n, 6)),
        dma((n,)), dma((n, 4)),
        dma((1 + len(LAST_DIRECT),)),
    ]
    return pl.pallas_call(
        kernel,
        out_shape=pltpu.VMEM((64, 3072), BF16),
        in_specs=[hbm] * 6,
        out_specs=vmem,
        scratch_shapes=scratch,
        compiler_params=pltpu.CompilerParams(collective_id=0, has_side_effects=True),
        name="contract",
    )(a_row_ids, a_col_ids, a_mask.T, b_mask, blocks, b_matrix)


def solution(mesh):
    return jax.shard_map(
        body,
        mesh=mesh,
        in_specs=(
            P("row", ("col", "depth"), None),
            P("row", ("col", "depth")),
            P(),
            P(),
            P(("row", "depth"), "col"),
            P(("row", "depth"), "col"),
        ),
        out_specs=P(("row", "depth"), "col"),
        check_vma=False,
    )
```

time: 273 us -> 54.1 us (0.20)
  waiting for transfers between devices: 197 us -> 0 us
  Pallas kernels: 0 us -> 53.2 us
  starting transfers between devices: 22.9 us -> 0 us
  other arithmetic: 21.8 us -> 0 us
  local copies, waits for them, and re-layouts: 17.9 us -> 0.75 us
  matrix products: 11.5 us -> 0 us
    ppermute x10 -> x0, waiting for transfers between devices: 179 us -> none  [the longest x7 167 us: partner(): return lax.ppermute(value, axis, pairs)]
    pallas_call x0 -> x1, Pallas kernels: none -> 53.2 us  [body(): pl.pallas_call(kernel, out_shape=pltpu.VMEM((64, 3072), BF16), in_specs=[...]
    ppermute x10 -> x0, starting transfers between devices: 18.5 us -> none  [the longest x7 16.8 us: partner(): return lax.ppermute(value, axis, pairs)]
    all_to_all x1 -> x0, waiting for transfers between devices: 18.1 us -> none  [body(): lax.all_to_all(outgoing.reshape(grid_size * grid_size, capacity, -1), ('r...]
    dot_general x4 -> x0, matrix products: 11.5 us -> none  [the longest x1 3.69 us: advance(): jnp.dot(left_now, right_now, preferred_element_type=jnp.float32)]
    select_n x9 -> x0, other arithmetic: 8.32 us -> none  [the longest x2 3.63 us: body(): jnp.where(upper_bit, jnp.concatenate([received, right_tile], axis=0), jnp...]
    reshape x6 -> x0, local copies, waits for them, and re-layouts: 8.23 us -> none  [the longest x1 2.7 us: body(): incoming = incoming.reshape(slot_total, -1)]
    add x5 -> x0, other arithmetic: 6.18 us -> none  [the longest x2 6.15 us: body(): running_sum = kept_half + received]
  transfers between devices with their start and end apart: 11 -> 0, of which waited for: 9 -> 0; matrix products, arithmetic and copies ran while one was open for 9% -> 0% of each run, Pallas kernels for 0% -> 0%
where the time goes in v2:
time: 54.1 us; the launch traced here: 54 us
  Pallas kernels  53.2 us (98%)
  local copies, waits for them, and re-layouts  0.75 us (1%)
    pallas_call x1, Pallas kernels, body(): pl.pallas_call(kernel, out_shape=pltpu.VMEM((64, 3072), BF16), in_specs=[...  53.2 us

profile of v2, /device:TPU:0, one launch (start us, length us, event | category | flops | bytes accessed | tf_op | source)
XLA Modules:
  0.0 54.0 jit_solution(11836766135861084975)
XLA Ops:
  0.0 53.2 %contract.1 = bf16[64,3072]{1,0:T(8,128)(2,1)S(1)} custom-call(s32[64]{0:T(128)} %rowid_hbm.1, s32[128]{0:T(128)} %colid_hbm.1, s32[2,32]{1,0:T(2,128)} %bitcast.7, s32[2,48]{1,0:T(2,128)} %bmask_hbm.1, bf16[32,64,128]{2,1,0:T(8,128)(2,1)} %bitcast.6, bf16[128,3072]{1,0:T(8,128)(2,1)} %b_hbm.1), custom_call_target="tpu_custom_call" | custom-call | tf_op jit(solution)/shard_map/contract/pallas_call | solution.py:395
  53.2 0.7 %copy.9 = bf16[64,3072]{1,0:T(8,128)(2,1)} copy(bf16[64,3072]{1,0:T(8,128)(2,1)S(1)} %contract.1) | data formatting | bytes 786432

commit v3 on v2

--- a/solution.py
+++ b/solution.py
@@ -12,6 +12,7 @@
 A_DIRECT = ()
 B_DIRECT = ()
 LAST_DIRECT = (5, 6)
+ALL_DIRECT = ()
 HALF = 1536
 F32 = jnp.float32
 BF16 = jnp.bfloat16
@@ -20,27 +21,27 @@
 C_FAR, C_NEAR, C_PRE, C_COMB, C_OWN, C_FINAL, C_LAST = range(12, 19)
 
 ORDER = (
-    (B_OWN, 3), (B_PAIR, 0), (AX,), (B_OWN, 0), (B_PAIR, 3), (A_PREP, 0, 2), (A_PREP, 0, 1), (A_PREP, 0, 3),
-    (B_PAIR, 1), (A_PREP, 0, 0), (A_PREP, 1, 2), (A_PREP, 1, 1), (B_PAIR, 4), (A_PREP, 1, 3), (A_PREP, 2, 2),
-    (B_MID, 3, 0), (A_PREP, 1, 0), (B_OTHER, 3), (A_RING, 0, 1), (B_OWN, 1), (A_RING, 0, 3), (A_RING, 0, 2),
-    (B_OTHER, 1), (A_RING, 1, 2), (A_PREP, 2, 1), (A_RING, 1, 3), (A_RING, 1, 1), (B_MID, 3, 1), (A_FWD, 0, 1),
-    (B_PAIR, 2), (A_FWD, 1, 0), (A_FWD, 0, 2), (A_PREP, 2, 3), (B_OTHER, 0), (A_FWD, 0, 0), (B_MID, 1, 1),
-    (A_FWD, 0, 3), (B_MID, 1, 0), (A_FWD, 1, 3), (A_FWD, 1, 2), (A_PREP, 3, 2), (A_FWD, 1, 1), (A_PREP, 3, 1),
-    (A_PREP, 2, 0), (A_PREP, 3, 3), (A_RING, 2, 2), (B_FAR, 3), (B_SIDE, 3), (A_RING, 2, 1), (B_SIDE, 1),
-    (B_READY, 3), (A_RING, 2, 3), (B_PAIR, 5), (B_MID, 0, 0), (A_READY, 0), (B_MID, 0, 1), (B_OWN, 2), (C_FAR, 3),
-    (A_FWD, 2, 0), (A_READY, 1), (B_FAR, 1), (B_PAIR, 6), (C_NEAR, 3), (A_FWD, 2, 1), (B_SIDE, 0), (A_FWD, 2, 2),
-    (B_OTHER, 2), (B_READY, 1), (C_FAR, 1), (A_FWD, 2, 3), (C_NEAR, 1), (B_OWN, 4), (B_OTHER, 4), (A_RING, 3, 3),
-    (A_PREP, 3, 0), (A_RING, 3, 2), (B_FAR, 0), (B_MID, 2, 0), (B_READY, 0), (C_FAR, 0), (C_NEAR, 0), (A_RING, 3, 1),
-    (A_READY, 2), (C_PRE, 3), (C_PRE, 1), (B_MID, 2, 1), (C_COMB, 3, 0), (B_OTHER, 6), (C_COMB, 3, 1), (C_COMB, 1, 1),
-    (B_OWN, 6), (A_FWD, 3, 3), (B_SIDE, 2), (A_FWD, 3, 0), (C_COMB, 1, 0), (C_PRE, 0), (A_FWD, 3, 1), (A_FWD, 3, 2),
-    (B_MID, 4, 1), (B_MID, 4, 0), (C_COMB, 0, 1), (C_COMB, 0, 0), (B_FAR, 2), (B_OWN, 5), (B_OTHER, 5), (B_SIDE, 4),
-    (B_READY, 2), (B_MID, 6, 0), (C_FAR, 2), (B_MID, 6, 1), (A_READY, 3), (C_OWN, 3), (B_SIDE, 6), (C_FINAL, 3),
-    (C_OWN, 1), (B_FAR, 4), (C_OWN, 0), (C_NEAR, 2), (C_PRE, 2), (C_FINAL, 1), (B_MID, 5, 0), (B_MID, 5, 1),
-    (B_READY, 4), (C_FAR, 4), (C_FINAL, 0), (B_FAR, 6), (C_COMB, 2, 1), (C_COMB, 2, 0), (B_SIDE, 5), (C_OWN, 2),
-    (B_READY, 6), (C_OWN, 6), (C_PRE, 4), (C_FAR, 6), (C_PRE, 6), (B_FAR, 5), (C_NEAR, 4), (B_READY, 5), (C_FAR, 5),
-    (C_COMB, 4, 0), (C_COMB, 4, 1), (C_OWN, 5), (C_OWN, 4), (C_FINAL, 2), (C_LAST, 1), (C_COMB, 6, 0), (C_COMB, 6, 1),
-    (C_LAST, 3), (C_NEAR, 5), (C_PRE, 5), (C_COMB, 5, 1), (C_LAST, 0), (C_NEAR, 6), (C_COMB, 5, 0), (C_LAST, 2),
-    (C_FINAL, 4), (C_FINAL, 5), (C_LAST, 4), (C_FINAL, 6),
+    (B_OWN, 3), (B_PAIR, 3), (AX,), (B_PAIR, 1), (B_OWN, 0), (A_PREP, 0, 2), (A_PREP, 0, 1), (A_PREP, 0, 3),
+    (A_PREP, 0, 0), (A_PREP, 1, 2), (A_PREP, 1, 1), (A_PREP, 1, 3), (B_PAIR, 0), (B_OTHER, 3), (B_PAIR, 2),
+    (B_OWN, 1), (A_PREP, 1, 0), (A_RING, 0, 1), (A_RING, 0, 2), (B_OTHER, 1), (A_RING, 0, 3), (A_PREP, 2, 2),
+    (A_RING, 1, 3), (A_RING, 1, 1), (B_MID, 3, 0), (A_RING, 1, 2), (B_PAIR, 4), (A_FWD, 0, 0), (B_MID, 3, 1),
+    (A_PREP, 2, 1), (B_MID, 1, 0), (A_FWD, 0, 1), (B_OTHER, 0), (A_FWD, 0, 3), (A_FWD, 0, 2), (A_FWD, 1, 0),
+    (A_PREP, 2, 3), (B_MID, 1, 1), (B_SIDE, 3), (A_FWD, 1, 3), (A_FWD, 1, 1), (A_PREP, 2, 0), (A_PREP, 3, 2),
+    (A_FWD, 1, 2), (B_MID, 0, 0), (A_PREP, 3, 1), (A_PREP, 3, 3), (B_SIDE, 1), (B_FAR, 3), (A_RING, 2, 2),
+    (A_RING, 2, 1), (B_MID, 0, 1), (A_READY, 0), (A_RING, 2, 3), (B_OWN, 2), (B_READY, 3), (C_FAR, 3), (A_PREP, 3, 0),
+    (B_FAR, 1), (B_SIDE, 0), (A_READY, 1), (B_OTHER, 2), (B_OWN, 4), (C_NEAR, 3), (B_PAIR, 6), (A_FWD, 2, 0),
+    (A_FWD, 2, 2), (A_FWD, 2, 1), (B_READY, 1), (C_FAR, 1), (A_FWD, 2, 3), (B_FAR, 0), (C_NEAR, 1), (A_RING, 3, 2),
+    (A_RING, 3, 3), (B_OTHER, 4), (A_FWD, 3, 0), (A_RING, 3, 1), (B_PAIR, 5), (B_READY, 0), (C_FAR, 0), (B_MID, 2, 0),
+    (C_NEAR, 0), (B_MID, 2, 1), (A_READY, 2), (C_PRE, 3), (C_PRE, 1), (C_COMB, 3, 1), (C_COMB, 1, 1), (B_OWN, 6),
+    (C_COMB, 3, 0), (B_MID, 4, 0), (A_FWD, 3, 2), (C_COMB, 1, 0), (B_OTHER, 6), (C_PRE, 0), (B_SIDE, 2),
+    (A_FWD, 3, 3), (B_MID, 4, 1), (B_OTHER, 5), (A_FWD, 3, 1), (B_OWN, 5), (C_COMB, 0, 1), (B_SIDE, 4),
+    (C_COMB, 0, 0), (B_FAR, 2), (B_MID, 6, 0), (B_MID, 6, 1), (B_READY, 2), (C_FAR, 2), (A_READY, 3), (C_OWN, 3),
+    (C_OWN, 2), (C_FINAL, 3), (B_FAR, 4), (C_OWN, 1), (C_NEAR, 2), (B_MID, 5, 1), (C_OWN, 0), (C_FINAL, 1),
+    (B_MID, 5, 0), (B_READY, 4), (C_FAR, 4), (B_SIDE, 6), (C_FINAL, 0), (B_FAR, 6), (B_SIDE, 5), (C_PRE, 2),
+    (C_PRE, 4), (C_COMB, 2, 1), (C_COMB, 2, 0), (B_READY, 6), (C_FAR, 6), (B_FAR, 5), (C_NEAR, 4), (C_LAST, 0),
+    (C_OWN, 6), (B_READY, 5), (C_FAR, 5), (C_COMB, 4, 1), (C_COMB, 4, 0), (C_PRE, 6), (C_OWN, 5), (C_FINAL, 2),
+    (C_COMB, 6, 0), (C_COMB, 6, 1), (C_NEAR, 6), (C_NEAR, 5), (C_PRE, 5), (C_COMB, 5, 1), (C_OWN, 4), (C_COMB, 5, 0),
+    (C_LAST, 3), (C_FINAL, 4), (C_LAST, 1), (C_FINAL, 6), (C_LAST, 2), (C_LAST, 4), (C_FINAL, 5),
 )
 
 
@@ -87,6 +88,8 @@
     peers = [dev_y(1), dev_y(2), dev_y(3), dev_z(1), dev_z(3), part, other, sib] + ([far] if A_DIRECT else [])
     if LAST_DIRECT:
         peers += [dev(x_part, y, lax.rem(z + 1, 4)), dev(x_part, y, lax.rem(z + 3, 4))]
+    if ALL_DIRECT:
+        peers += [dev_z(2), dev(x_part, y, lax.rem(z + 2, 4))]
     for peer in peers:
         pl.semaphore_signal(barrier, inc=1, device_id=peer, device_id_type=MESH)
 
@@ -115,18 +118,9 @@
     to_smem = pltpu.make_async_copy(slotv, slot_ref, slot_sem)
     to_smem.start()
 
-    for load in loads[3:]:
-        load.wait()
-    pl.semaphore_wait(barrier, len(peers))
     left_lane = lax.broadcasted_iota(jnp.int32, (64, 128), 1) < 64
     own_plane = y * 2 + l
     two = pl.ds(r * 2, 2)
-    exchange = []
-
-    def ax():
-        mine = pl.ds(r * 32, 32)
-        exchange.append(rcopy(araw.at[mine], araw.at[mine], sx_s, sx_r, sib))
-        to_smem.wait()
 
     def mask_b(ch, half):
         start = sum(CHUNKS[:ch])
@@ -138,6 +132,30 @@
                 tile = b_ref[pl.ds(j * 64, 64), pl.ds(pl.multiple_of(col, 128), 128)].astype(F32)
                 yield j, t, (tile * factor).astype(BF16)
 
+    def prep_pair(ch):
+        for j, t, tile in mask_b(ch, 1 - l):
+            bxs[ch][j, :, pl.ds(t * 128, 128)] = tile
+
+    def prep_own(ch):
+        for j, t, tile in mask_b(ch, l):
+            bbuf[ch][own_plane, r * 2 + j, :, pl.ds(t * 128, 128)] = tile
+
+    for load in loads[3:]:
+        load.wait()
+    early = ORDER[: ORDER.index((A_PREP, 0, 2))]
+    for step, *where in early:
+        if step == B_PAIR:
+            prep_pair(*where)
+        if step == B_OWN:
+            prep_own(*where)
+    pl.semaphore_wait(barrier, len(peers))
+    exchange = []
+
+    def ax():
+        mine = pl.ds(r * 32, 32)
+        exchange.append(rcopy(araw.at[mine], araw.at[mine], sx_s, sx_r, sib))
+        to_smem.wait()
+
     def piece(ch, k, lam):
         plane = lax.rem(y + k, 4) * 2 + (l if lam == 0 else 1 - l)
         return bbuf[ch].at[plane, two]
@@ -149,16 +167,16 @@
         bytes_of(rbuf[ch].at[pl.ds(0, 128 * pieces)], sb_s.at[ch], sb_r.at[ch, i]).wait_recv()
 
     def b_pair(ch):
-        for j, t, tile in mask_b(ch, 1 - l):
-            bxs[ch][j, :, pl.ds(t * 128, 128)] = tile
+        if (B_PAIR, ch) not in early:
+            prep_pair(ch)
         rcopy(bxs[ch], bbuf[ch].at[own_plane, two], sb_s.at[ch], sb_r.at[ch, 0], part)
 
     def b_own(ch):
-        for j, t, tile in mask_b(ch, l):
-            bbuf[ch][own_plane, r * 2 + j, :, pl.ds(t * 128, 128)] = tile
+        if (B_OWN, ch) not in early:
+            prep_own(ch)
         b_copy(ch, 1, piece(ch, 0, 0), dev_y(1))
         b_copy(ch, 3, piece(ch, 0, 0), dev_y(3))
-        if ch in B_DIRECT:
+        if (ch, 0) in B_DIRECT:
             b_copy(ch, 4, piece(ch, 0, 0), dev_y(2))
         b_copy(ch, 5, piece(ch, 0, 0), sib)
 
@@ -166,14 +184,14 @@
         b_wait(ch, 0, 1)
         b_copy(ch, 3, piece(ch, 0, 1), dev_y(1))
         b_copy(ch, 2, piece(ch, 0, 1), dev_y(3))
-        if ch in B_DIRECT:
+        if (ch, 1) in B_DIRECT:
             b_copy(ch, 4, piece(ch, 0, 1), dev_y(2))
         b_copy(ch, 5, piece(ch, 0, 1), sib)
 
     def b_mid(ch, lam):
         b_wait(ch, 1 + lam, 1)
         ref = piece(ch, 3 - 2 * lam, lam)
-        if ch not in B_DIRECT:
+        if (ch, lam) not in B_DIRECT:
             b_copy(ch, 4, ref, dev_y(1 + 2 * lam))
         b_copy(ch, 5, ref, sib)
 
@@ -234,7 +252,7 @@
 
     def a_send(g, k):
         ref = held(g, x, k)
-        onward = g not in A_DIRECT
+        onward = (g, k) not in A_DIRECT
         a_copy(g, 3 + k if onward and k in BY_OTHER else 7, ref, ref, part)
         a_copy(g, 3 + k if onward and k not in BY_OTHER else 7, ref, ref, other)
         if not onward:
@@ -251,11 +269,14 @@
         a_copy(g, 7, ref, ref, target)
 
     def a_ready(g):
-        a_wait(g, 7, 12 if g in A_DIRECT else 8)
+        a_wait(g, 7, 8 + sum((g, k) in A_DIRECT for k in range(4)))
 
     def multiply(ch, g):
-        lhs = jnp.concatenate([abuf[g][i] for i in range(16)], axis=1)
-        total = jnp.dot(lhs, rbuf[ch][...], preferred_element_type=F32)
+        total = None
+        for k in range(0, 16, 4):
+            lhs = jnp.concatenate([abuf[g][i] for i in range(k, k + 4)], axis=1)
+            share = jnp.dot(lhs, rbuf[ch][pl.ds(k * 128, 512), :], preferred_element_type=F32)
+            total = share if total is None else total + share
         for n, unit in enumerate(GROUPS[g]):
             cp[ch][unit] = total[n * 64 : n * 64 + 64]
 
@@ -268,22 +289,29 @@
     def last_copy(ch, src, kind, target):
         rcopy(src, last[LAST_DIRECT.index(ch)].at[kind, l], sc_s.at[ch], sc_r.at[ch, 2], target)
 
+    def straight(ch, g):
+        for zr, h in GROUPS[g]:
+            last_copy(ch, cp[ch].at[zr, h], zr - 1, dev(c * 2 + h, y, lax.rem(z + zr, 4)))
+
     def c_far(ch):
         multiply(ch, 0)
+        if ch in ALL_DIRECT:
+            return straight(ch, 0)
         c_copy(ch, 0, cp[ch].at[2, 0], rsin[ch].at[0], dev_z(1))
         c_copy(ch, 1, cp[ch].at[2, 1], rsin[ch].at[1], dev_z(3))
 
     def c_near(ch):
         multiply(ch, 1)
         if ch in LAST_DIRECT:
-            last_copy(ch, cp[ch].at[1, 1], 0, dev(c * 2 + 1, y, lax.rem(z + 1, 4)))
-            last_copy(ch, cp[ch].at[3, 0], 0, dev(c * 2, y, lax.rem(z + 3, 4)))
+            straight(ch, 1)
         else:
             c_copy(ch, 2, cp[ch].at[1, 1], rsin[ch].at[2], dev_z(1))
             c_copy(ch, 2, cp[ch].at[3, 0], rsin[ch].at[3], dev_z(3))
 
     def c_pre(ch):
         multiply(ch, 2)
+        if ch in ALL_DIRECT:
+            straight(ch, 2)
 
     def c_comb(ch, n):
         c_wait(ch, n, cp[ch].at[0, 0])
@@ -296,7 +324,7 @@
     def c_own(ch):
         multiply(ch, 3)
         if ch in LAST_DIRECT:
-            rcopy(cp[ch].at[0, 1 - l], last[LAST_DIRECT.index(ch)].at[2, l], sf_s.at[1 + LAST_DIRECT.index(ch)], sc_r.at[ch, 3], part)
+            rcopy(cp[ch].at[0, 1 - l], last[LAST_DIRECT.index(ch)].at[3, l], sf_s.at[1 + LAST_DIRECT.index(ch)], sc_r.at[ch, 3], part)
 
     def out_half(ch, s, h):
         for t in range(CHUNKS[ch] // 128):
@@ -311,11 +339,15 @@
 
     def c_final_direct(ch):
         at = LAST_DIRECT.index(ch)
-        c_wait(ch, 2, cp[ch].at[pl.ds(0, 2)])
+        c_wait(ch, 2, cp[ch].at[pl.ds(0, 3 if ch in ALL_DIRECT else 2)])
         c_wait(ch, 3, cp[ch].at[0, 0])
         for n, s in enumerate((l, 1 - l)):
-            own = last[at][2, s] if n else cp[ch][0, l]
-            interleave(ch, n, own + last[at][0, s] + last[at][1, s])
+            value = last[at][3, s] if n else cp[ch][0, l]
+            if ch in ALL_DIRECT:
+                value += last[at][0, s] + last[at][2, s]
+            else:
+                value += last[at][2 * (1 - l), s]
+            interleave(ch, n, value + last[at][1, s])
             out_half(ch, s, n)
 
     def c_final(ch):
@@ -385,7 +417,7 @@
         [pltpu.VMEM((2, w // 128, 64, 128), F32) for w in CHUNKS],
         [pltpu.VMEM((64, w), BF16) for w in CHUNKS],
         [pltpu.VMEM((64, w), BF16) for w in CHUNKS],
-        [pltpu.VMEM((3, 2, 64, CHUNKS[ch]), F32) for ch in LAST_DIRECT],
+        [pltpu.VMEM((4, 2, 64, CHUNKS[ch]), F32) for ch in LAST_DIRECT],
         dma, dma, dma,
         dma((groups,)), dma((groups, 8)),
         dma((n,)), dma((n, 6)),

time: 54.1 us -> 54.3 us (level)
  no operation moved by 1% of the time
where the time goes in v3:
time: 54.3 us; the launch traced here: 54 us
  Pallas kernels  53.2 us (98%)
  local copies, waits for them, and re-layouts  0.75 us (1%)
    pallas_call x1, Pallas kernels, body(): pl.pallas_call(kernel, out_shape=pltpu.VMEM((64, 3072), BF16), in_specs=[...  53.2 us

profile of v3, /device:TPU:0, one launch (start us, length us, event | category | flops | bytes accessed | tf_op | source)
XLA Modules:
  0.0 54.0 jit_solution(11426034226786712355)
XLA Ops:
  0.0 53.2 %contract.1 = bf16[64,3072]{1,0:T(8,128)(2,1)S(1)} custom-call(s32[64]{0:T(128)} %rowid_hbm.1, s32[128]{0:T(128)} %colid_hbm.1, s32[2,32]{1,0:T(2,128)} %bitcast.7, s32[2,48]{1,0:T(2,128)} %bmask_hbm.1, bf16[32,64,128]{2,1,0:T(8,128)(2,1)} %bitcast.6, bf16[128,3072]{1,0:T(8,128)(2,1)} %b_hbm.1), custom_call_target="tpu_custom_call" | custom-call | tf_op jit(solution)/shard_map/contract/pallas_call | solution.py:427
  53.2 0.7 %copy.9 = bf16[64,3072]{1,0:T(8,128)(2,1)} copy(bf16[64,3072]{1,0:T(8,128)(2,1)S(1)} %contract.1) | data formatting | bytes 786432
